TPU v7x, 128 devices: a whole 4x4x4 slice. The times are simulated.
128 devices in a mesh: dp: 8 (over z_hi, x), section: 4 (over y), tensor: 4 (over z_lo, core).
Axes of the slice: x: 4, y: 4, z: 4 (z_hi: 2, z_lo: 2; z = z_hi * 2 + z_lo), core: 2. Of those that a mesh axis runs over, the one named last changes fastest.
Arguments:
- failed_section: int32 [8], P('dp'), may hold values from 0 to 999
- token_ids: int32 [8, 2048], P('dp'), may hold values from 0 to 100001, as said below
- section_outputs: bfloat16 [8, 4, 2048, 2048], P('dp', 'section', None, 'tensor'), may hold values from -11 to 11
- w_query: float32 [4, 2048, 1024], P('section', 'dp', 'tensor'), may hold values from -1 to 1
- w_key: float32 [4, 2048, 1024], P('section', 'dp', 'tensor'), may hold values from -2 to 2
- w_value: float32 [4, 2048, 1024], P('section', 'dp', 'tensor'), may hold values from -0.125 to 0.125
- w_out: float32 [4, 2048, 1024], P('section', 'dp', 'tensor'), may hold values from -0.75 to 0.75
- m_value: float32 [4, 2048, 1024], P('section', 'dp', 'tensor'), may hold values from -3 to 3
- v_value: float32 [4, 2048, 1024], P('section', 'dp', 'tensor'), may hold values from 0.001 to 1
- m_out: float32 [4, 2048, 1024], P('section', 'dp', 'tensor'), may hold values from -3 to 3
- v_out: float32 [4, 2048, 1024], P('section', 'dp', 'tensor'), may hold values from 0.001 to 1
Outputs:
- restored_query: float32 [8, 4, 2048, 1024], P('dp', 'section', None, 'tensor')
- restored_key: float32 [8, 4, 2048, 1024], P('dp', 'section', None, 'tensor')
- restored_value: float32 [8, 4, 2048, 1024], P('dp', 'section', None, 'tensor')
- restored_out: float32 [8, 4, 2048, 1024], P('dp', 'section', None, 'tensor')
- restored_m_value: float32 [8, 4, 2048, 1024], P('dp', 'section', None, 'tensor')
- restored_v_value: float32 [8, 4, 2048, 1024], P('dp', 'section', None, 'tensor')
- restored_m_out: float32 [8, 4, 2048, 1024], P('dp', 'section', None, 'tensor')
- restored_v_out: float32 [8, 4, 2048, 1024], P('dp', 'section', None, 'tensor')
- attn_update: bfloat16 [8, 4, 2048, 2048], P('dp', 'section', None, 'tensor')
Inputs may be any that keep to these rules, and one draw needn't show every extreme that they name: `token_ids`: token ids of each replica's micro-batch; the id 100001 ends a document, the others are ordinary tokens below 100000.
All inputs are finite; a program needn't handle non-finite values.
Results may differ from a plain program's by a relative error of at most 0.0087.
Values may be sent and summed in bfloat16 or wider, within the bound.
A program may use at most 128 MiB of HBM per device.

v0:
```python
import math
import jax
import jax.numpy as jnp
from jax import lax
from jax.sharding import PartitionSpec as P

HD = 128
end_token = 100001
mask_fill = -1e30


def sent_together(arrays, axis, dim, along):
    ends, at = ([], 0)
    for a in arrays[:-1]:
        at += a.shape[along]
        ends.append(at)
    both = jnp.concatenate(arrays, axis=along)
    return tuple(jnp.split(lax.all_gather(both, axis, axis=dim, tiled=True), ends, axis=along))


def passed_along(array, axis, by):
    count = lax.axis_size(axis)
    return lax.ppermute(array, axis, [(i, (i + by) % count) for i in range(count)])


def document_ids(token_row):
    doc_ends = (token_row == end_token).astype(jnp.int32)
    return jnp.cumsum(doc_ends) - doc_ends


def attend(queries, key_vals, value_vals, token_row):
    token_count = queries.shape[0]
    heads_local = queries.shape[1] // HD
    block_rows = min(512, token_count)
    document = document_ids(token_row)
    positions = jnp.arange(token_count, dtype=jnp.int32)
    key_heads = key_vals.reshape(token_count, heads_local, HD)
    value_heads = value_vals.reshape(token_count, heads_local, HD)

    def one_block(block_index):
        first_row = block_index * block_rows
        query_block = lax.dynamic_slice_in_dim(queries, first_row, block_rows, 0).reshape(
            block_rows, heads_local, HD
        )
        scores = jnp.einsum(
            "qhd,khd->hqk", query_block, key_heads, preferred_element_type=jnp.float32
        ) * (1.0 / math.sqrt(HD))
        query_pos = lax.dynamic_slice_in_dim(positions, first_row, block_rows, 0)
        query_doc = lax.dynamic_slice_in_dim(document, first_row, block_rows, 0)
        allowed = (positions[None, :] <= query_pos[:, None]) & (
            document[None, :] == query_doc[:, None]
        )
        scores = jnp.where(allowed[None], scores, mask_fill)
        highest = jnp.max(scores, axis=2, keepdims=True)
        weights = jnp.exp(scores - highest)
        probs = (weights / jnp.sum(weights, axis=2, keepdims=True)).astype(jnp.bfloat16)
        context = jnp.einsum(
            "hqk,khd->qhd", probs, value_heads, preferred_element_type=jnp.float32
        ).astype(jnp.bfloat16)
        return context.reshape(block_rows, heads_local * HD)

    blocks = lax.map(one_block, jnp.arange(token_count // block_rows, dtype=jnp.int32))
    return blocks.reshape(token_count, heads_local * HD)


def shards(
    failed_section,
    token_ids,
    section_outputs,
    w_query,
    w_key,
    w_value,
    w_out,
    m_value,
    v_value,
    m_out,
    v_out,
):
    section_failed = jnp.remainder(failed_section[0], lax.axis_size("section"))
    replacing = lax.axis_index("section") == section_failed
    masters = tuple(
        (
            part.astype(jnp.float32)
            for part in sent_together(
                (
                    w_query.astype(jnp.bfloat16),
                    w_key.astype(jnp.bfloat16),
                    w_value.astype(jnp.bfloat16),
                    w_out.astype(jnp.bfloat16),
                ),
                "dp",
                1,
                0,
            )
        )
    )
    query_bf = masters[0][0].astype(jnp.bfloat16)
    key_bf = masters[1][0].astype(jnp.bfloat16)
    value_bf = masters[2][0].astype(jnp.bfloat16)
    out_bf = masters[3][0].astype(jnp.bfloat16)
    inner_local = query_bf.shape[1]
    w_joined = jnp.concatenate([query_bf, key_bf, value_bf], axis=1)
    incoming = passed_along(section_outputs, "section", 1)
    projected = jnp.dot(
        lax.all_gather(incoming, "tensor", axis=3, tiled=True)[0, 0],
        w_joined,
        preferred_element_type=jnp.float32,
    )
    queries = projected[:, :inner_local].astype(jnp.bfloat16)
    key_vals = projected[:, inner_local : 2 * inner_local].astype(jnp.bfloat16)
    value_vals = projected[:, 2 * inner_local :].astype(jnp.bfloat16)
    context = attend(queries, key_vals, value_vals, token_ids[0])
    context_whole = lax.all_gather(context, "tensor", axis=1, tiled=True)
    out_slice = lax.all_to_all(out_bf, "tensor", split_axis=0, concat_axis=1, tiled=True)
    update = lax.dot_general(
        context_whole, out_slice, (((1,), (1,)), ((), ())), preferred_element_type=jnp.float32
    ).astype(jnp.bfloat16)
    moments = tuple(
        (
            part.astype(jnp.float32)
            for part in sent_together(
                (
                    m_value.astype(jnp.bfloat16),
                    v_value.astype(jnp.bfloat16),
                    m_out.astype(jnp.bfloat16),
                    v_out.astype(jnp.bfloat16),
                ),
                "dp",
                1,
                0,
            )
        )
    )

    def placed(gathered):
        return jnp.where(replacing, gathered[None], jnp.zeros_like(gathered[None]))

    update_block = jnp.where(
        replacing, update[None, None], jnp.zeros((1, 1) + update.shape, jnp.bfloat16)
    )
    return (
        placed(masters[0]),
        placed(masters[1]),
        placed(masters[2]),
        placed(masters[3]),
        placed(moments[0]),
        placed(moments[1]),
        placed(moments[2]),
        placed(moments[3]),
        update_block,
    )


def solution(mesh):
    return jax.shard_map(
        shards,
        mesh=mesh,
        in_specs=(
            P("dp"),
            P("dp", None),
            P("dp", "section", None, "tensor"),
            P("section", "dp", "tensor"),
            P("section", "dp", "tensor"),
            P("section", "dp", "tensor"),
            P("section", "dp", "tensor"),
            P("section", "dp", "tensor"),
            P("section", "dp", "tensor"),
            P("section", "dp", "tensor"),
            P("section", "dp", "tensor"),
        ),
        out_specs=(
            P("dp", "section", None, "tensor"),
            P("dp", "section", None, "tensor"),
            P("dp", "section", None, "tensor"),
            P("dp", "section", None, "tensor"),
            P("dp", "section", None, "tensor"),
            P("dp", "section", None, "tensor"),
            P("dp", "section", None, "tensor"),
            P("dp", "section", None, "tensor"),
            P("dp", "section", None, "tensor"),
        ),
        check_vma=False,
    )
```

profile of v0, /device:TPU:1, one launch (start us, length us, event | category | flops | bytes accessed | tf_op | source)
XLA Modules:
  0.0 302.3 jit_solution(5347417715151155394)
XLA Ops:
  7.3 1.0 convert_element_type.92
  8.3 1.0 convert_element_type.93
  12.2 2.2 collective-permute-start
  14.3 47.0 %collective-permute-done = bf16[1,1,2048,512]{3,2,1,0:T(8,128)(2,1)S(1)} collective-permute-done((bf16[1,1,2048,512]{3,2,1,0:T(8,128)(2,1)}, bf16[1,1,2048,512]{3,2,1,0:T(8,128)(2,1)S(1)}, u32[]{:S(2)}, u32[]{:S(2)}) %collective-permute-start) | collective-permute-done | bytes 2097184 | tf_op jit(solution)/shard_map/ppermute | solution.py:23
  61.3 1.3 copy-done
  64.4 21.9 %all-gather.5.cloned.1.call-done = bf16[4,2048,256]{2,1,0:T(8,128)(2,1)} async-done(((bf16[4,256,256]{2,1,0:T(8,128)(2,1)}), bf16[4,2048,256]{2,1,0:T(8,128)(2,1)}) %all-gather.5.cloned.1.call-update) | async-done | bytes 4194320 | tf_op jit(solution)/shard_map/all_gather | solution.py:18
  86.3 3.4 %fusion.30 = (bf16[1,2048,256]{2,1,0:T(8,128)(2,1)}, bf16[2048,256]{1,0:T(8,128)(2,1)S(1)}, bf16[2048,256]{1,0:T(8,128)(2,1)S(1)}, bf16[2048,256]{1,0:T(8,128)(2,1)S(1)}) fusion(bf16[4,2048,256]{2,1,0:T(8,128)(2,1)} %all-gather.5.cloned.1.call-done), kind=kLoop, calls=%fused_computation.46 | loop fusion | bytes 8388608 | tf_op jit(solution)/shard_map/split | solution.py:18
  89.7 79.1 %all-gather.9.cloned.1.call-done = bf16[1,1,2048,2048]{3,2,1,0:T(8,128)(2,1)} async-done(((bf16[1,1,2048,512]{3,2,1,0:T(8,128)(2,1)}), bf16[1,1,2048,2048]{3,2,1,0:T(8,128)(2,1)}) %all-gather.9.cloned.1.call-update) | async-done | bytes 8388624 | tf_op jit(solution)/shard_map/all_gather | solution.py:105
  168.8 9.1 %fusion.21 = bf16[2048,768]{0,1:T(8,128)(2,1)S(1)} fusion(bf16[1,1,2048,2048]{3,2,1,0:T(8,128)(2,1)} %all-gather.9.cloned.1.call-done, bf16[2048,256]{1,0:T(8,128)(2,1)S(1)} %get-tuple-element.120, bf16[2048,256]{1,0:T(8,128)(2,1)S(1)} %get-tuple-element.119, bf16[2048,256]{1,0:T(8,128)(2,1)S(1)} %get-tuple-element.118), kind=kOutput, calls=%fused_computation.24 | convolution fusion | flops 6453460992 | bytes 14680064 | tf_op jit(solution)/shard_map/dot_general | solution.py:104
  178.0 1.2 fusion.31
  179.9 54.7 %while.11 = (s32[]{:T(128)}, bf16[4,512,256]{2,1,0:T(8,128)(2,1)}, s32[2048]{0:T(1024)S(1)}, s32[4]{0:T(128)S(1)}, s32[2048]{0:T(1024)S(1)}, /*index=5*/bf16[204...) while((s32[]{:T(128)}, bf16[4,512,256]{2,1,0:T(8,128)(2,1)}, ...), condition=%wide.region_5.6_spmd.clone, body=%wide.region_2.5_spmd.clone.sunk | while | flops 1089603584 | bytes 23106236 | solution.py:62
  182.3 5.2 %fusion.47 = (f32[2,512]{1,0:T(2,128)S(1)}, f32[2,512,2048]{2,1,0:T(8,128)}) fusion(pred[512,2048]{1,0:T(8,128)(4,1)S(1)} %compare_and_fusion.2, bf16[512,2,128]{0,2,1:T(8,128)(2,1)S(1)} %bitcast.71, bf16[2048,2,128]{2,0,1:T(8,128)(2,1)S(1)} %get-tuple-element.215), kind=kOutput, calls=%fused_computation.45.clone.1 | convolution fusion | flops 545261568 | bytes 10752000 | tf_op jit(solution)/shard_map/while/body/eval_jaxpr/sub | solution.py:55
  187.5 5.2 %fusion.48 = bf16[2,512,128]{1,2,0:T(8,128)(2,1)S(1)} fusion(bf16[2048,2,128]{0,2,1:T(8,128)(2,1)} %get-tuple-element.216, f32[2,512,2048]{2,1,0:T(8,128)} %get-tuple-element.183, f32[2,512]{1,0:T(2,128)S(1)} %get-tuple-element.184), kind=kOutput, calls=%fused_computation.10.clone.1 | convolution fusion | flops 541196288 | bytes 9703424 | tf_op jit(solution)/shard_map/while/body/eval_jaxpr/hqk,khd->qhd/dot_general | solution.py:57
  196.0 5.2 %fusion.47 = (f32[2,512]{1,0:T(2,128)S(1)}, f32[2,512,2048]{2,1,0:T(8,128)}) fusion(pred[512,2048]{1,0:T(8,128)(4,1)S(1)} %compare_and_fusion.2, bf16[512,2,128]{0,2,1:T(8,128)(2,1)S(1)} %bitcast.71, bf16[2048,2,128]{2,0,1:T(8,128)(2,1)S(1)} %get-tuple-element.215), kind=kOutput, calls=%fused_computation.45.clone.1 | convolution fusion | flops 545261568 | bytes 10752000 | tf_op jit(solution)/shard_map/while/body/eval_jaxpr/sub | solution.py:55
  201.2 5.2 %fusion.48 = bf16[2,512,128]{1,2,0:T(8,128)(2,1)S(1)} fusion(bf16[2048,2,128]{0,2,1:T(8,128)(2,1)} %get-tuple-element.216, f32[2,512,2048]{2,1,0:T(8,128)} %get-tuple-element.183, f32[2,512]{1,0:T(2,128)S(1)} %get-tuple-element.184), kind=kOutput, calls=%fused_computation.10.clone.1 | convolution fusion | flops 541196288 | bytes 9703424 | tf_op jit(solution)/shard_map/while/body/eval_jaxpr/hqk,khd->qhd/dot_general | solution.py:57
  209.6 5.2 %fusion.47 = (f32[2,512]{1,0:T(2,128)S(1)}, f32[2,512,2048]{2,1,0:T(8,128)}) fusion(pred[512,2048]{1,0:T(8,128)(4,1)S(1)} %compare_and_fusion.2, bf16[512,2,128]{0,2,1:T(8,128)(2,1)S(1)} %bitcast.71, bf16[2048,2,128]{2,0,1:T(8,128)(2,1)S(1)} %get-tuple-element.215), kind=kOutput, calls=%fused_computation.45.clone.1 | convolution fusion | flops 545261568 | bytes 10752000 | tf_op jit(solution)/shard_map/while/body/eval_jaxpr/sub | solution.py:55
  214.8 5.3 %fusion.48 = bf16[2,512,128]{1,2,0:T(8,128)(2,1)S(1)} fusion(bf16[2048,2,128]{0,2,1:T(8,128)(2,1)} %get-tuple-element.216, f32[2,512,2048]{2,1,0:T(8,128)} %get-tuple-element.183, f32[2,512]{1,0:T(2,128)S(1)} %get-tuple-element.184), kind=kOutput, calls=%fused_computation.10.clone.1 | convolution fusion | flops 541196288 | bytes 9703424 | tf_op jit(solution)/shard_map/while/body/eval_jaxpr/hqk,khd->qhd/dot_general | solution.py:57
  223.3 5.2 %fusion.47 = (f32[2,512]{1,0:T(2,128)S(1)}, f32[2,512,2048]{2,1,0:T(8,128)}) fusion(pred[512,2048]{1,0:T(8,128)(4,1)S(1)} %compare_and_fusion.2, bf16[512,2,128]{0,2,1:T(8,128)(2,1)S(1)} %bitcast.71, bf16[2048,2,128]{2,0,1:T(8,128)(2,1)S(1)} %get-tuple-element.215), kind=kOutput, calls=%fused_computation.45.clone.1 | convolution fusion | flops 545261568 | bytes 10752000 | tf_op jit(solution)/shard_map/while/body/eval_jaxpr/sub | solution.py:55
  228.5 5.2 %fusion.48 = bf16[2,512,128]{1,2,0:T(8,128)(2,1)S(1)} fusion(bf16[2048,2,128]{0,2,1:T(8,128)(2,1)} %get-tuple-element.216, f32[2,512,2048]{2,1,0:T(8,128)} %get-tuple-element.183, f32[2,512]{1,0:T(2,128)S(1)} %get-tuple-element.184), kind=kOutput, calls=%fused_computation.10.clone.1 | convolution fusion | flops 541196288 | bytes 9703424 | tf_op jit(solution)/shard_map/while/body/eval_jaxpr/hqk,khd->qhd/dot_general | solution.py:57
  235.3 3.7 %all-to-all-start = ((bf16[4,512,256]{2,1,0:T(8,128)(2,1)}), bf16[4,512,256]{2,1,0:T(8,128)(2,1)S(1)}, u32[]{:S(2)}, u32[]{:S(2)}) async-start(bf16[4,512,256]{2,1,0:T(8,128)(2,1)} %bitcast.20), calls=%async_computation | async-start | bytes 2097152 | tf_op jit(solution)/shard_map/all_to_all | solution.py:114
  239.0 5.7 %select_bitcast_fusion.4 = (f32[1,1,2048,256]{3,2,1,0:T(8,128)}, f32[1,1,2048,256]{3,2,1,0:T(8,128)}, f32[1,1,2048,256]{3,2,1,0:T(8,128)}, f32[1,1,2048,256]{3,2,1,0:T(8,128)}) fusion(pred[]{:T(512)S(6)} %eq.31, bf16[4,2048,256]{2,1,0:T(8,128)(2,1)} %all-gather.5.cloned.1.call-done), kind=kLoop, calls=%fused_computation.32 | loop fusion | flops 4194304 | bytes 12582913 | tf_op jit(solution)/shard_map/jit(_where)/select_n | solution.py:136
  244.7 5.7 %select_bitcast_fusion = (f32[1,1,2048,256]{3,2,1,0:T(8,128)}, f32[1,1,2048,256]{3,2,1,0:T(8,128)}, f32[1,1,2048,256]{3,2,1,0:T(8,128)}, f32[1,1,2048,256]{3,2,1,0:T(8,128)}) fusion(bf16[4,2048,256]{2,1,0:T(8,128)(2,1)} %all-gather.7.cloned.1.call-done, pred[]{:T(512)S(6)} %eq.31), kind=kLoop, calls=%fused_computation.28 | loop fusion | flops 4194304 | bytes 12582913 | tf_op jit(solution)/shard_map/jit(_where)/select_n | solution.py:136
  251.6 38.3 %all-gather.11.cloned.1.call-done = bf16[2048,1024]{1,0:T(8,128)(2,1)} async-done(((bf16[2048,256]{1,0:T(8,128)(2,1)}), bf16[2048,1024]{1,0:T(8,128)(2,1)}) %all-gather.11.cloned.1.call-update) | async-done | bytes 4194320 | tf_op jit(solution)/shard_map/all_gather | solution.py:113
  290.0 5.8 %fusion.27 = bf16[1,1,2048,512]{3,2,1,0:T(8,128)(2,1)} fusion(bf16[2048,1024]{1,0:T(8,128)(2,1)} %all-gather.11.cloned.1.call-done, bf16[512,1024]{0,1:T(8,128)(2,1)S(1)} %bitcast.76, pred[]{:T(512)S(6)} %eq.31), kind=kOutput, calls=%fused_computation.27 | convolution fusion | flops 2149580800 | bytes 7340033 | tf_op jit(solution)/shard_map/dot_general | solution.py:115
  (68 shorter events, 16.7 us)
Async XLA Ops:
  7.2 55.5 %copy-start.1 = (f32[1,256,256]{2,1,0:T(8,128)S(1)}, f32[1,256,256]{2,1,0:T(8,128)}, u32[]{:S(2)}) copy-start(f32[1,256,256]{2,1,0:T(8,128)} %param.20) | copy-start | bytes 786436
  7.2 55.6 %copy-start.2 = (f32[1,256,256]{2,1,0:T(8,128)S(1)}, f32[1,256,256]{2,1,0:T(8,128)}, u32[]{:S(2)}) copy-start(f32[1,256,256]{2,1,0:T(8,128)} %param.21) | copy-start | bytes 786436
  7.2 55.6 %copy-start.3 = (f32[1,256,256]{2,1,0:T(8,128)S(1)}, f32[1,256,256]{2,1,0:T(8,128)}, u32[]{:S(2)}) copy-start(f32[1,256,256]{2,1,0:T(8,128)} %param.22) | copy-start | bytes 786436
  7.2 55.6 %copy-start.4 = (f32[1,256,256]{2,1,0:T(8,128)S(1)}, f32[1,256,256]{2,1,0:T(8,128)}, u32[]{:S(2)}) copy-start(f32[1,256,256]{2,1,0:T(8,128)} %param.23) | copy-start | bytes 786436
  7.2 79.1 %all-gather.5.cloned.1.call-start = ((), (), s32[]{:S(2)}) async-start(), calls=%async_computation.1 | async-start | bytes 4718592 | tf_op jit(solution)/shard_map/all_gather | solution.py:18
  12.1 51.7 %copy-start.5 = (s32[1,2048]{1,0:T(1,128)S(1)}, s32[1,2048]{1,0:T(1,128)}, u32[]{:S(2)}) copy-start(s32[1,2048]{1,0:T(1,128)} %param.14) | copy-start | bytes 24580
  12.1 156.7 %all-gather.9.cloned.1.call-start = ((), (), s32[]{:S(2)}) async-start(), calls=%async_computation.3 | async-start | bytes 10485760 | tf_op jit(solution)/shard_map/all_gather | solution.py:105
  12.2 49.2 %collective-permute-start = (bf16[1,1,2048,512]{3,2,1,0:T(8,128)(2,1)}, bf16[1,1,2048,512]{3,2,1,0:T(8,128)(2,1)S(1)}, u32[]{:S(2)}, u32[]{:S(2)}) collective-permute-start(bf16[1,1,2048,512]{3,2,1,0:T(8,128)(2,1)} %param.15), channel_id=1, source_target_pairs={{0,4},{4,8},{8,12},{12,0},{1,5},{5,9},{9,13},{13,1},{2,6},{6,10},{... | collective-permute-start | bytes 6291464 | tf_op jit(solution)/shard_map/ppermute | solution.py:23
  61.3 1.3 copy-start
  62.7 182.0 %all-gather.7.cloned.1.call-start = ((), (), s32[]{:S(2)}) async-start(), calls=%async_computation.2 | async-start | bytes 4718592 | tf_op jit(solution)/shard_map/all_gather | solution.py:18
  63.7 226.2 %all-gather.11.cloned.1.call-start = ((), (), s32[]{:S(2)}) async-start(), calls=%async_computation.4 | async-start | bytes 5242880 | tf_op jit(solution)/shard_map/all_gather | solution.py:113
  235.3 15.8 %all-to-all-start = ((bf16[4,512,256]{2,1,0:T(8,128)(2,1)}), bf16[4,512,256]{2,1,0:T(8,128)(2,1)S(1)}, u32[]{:S(2)}, u32[]{:S(2)}) async-start(bf16[4,512,256]{2,1,0:T(8,128)(2,1)} %bitcast.20), calls=%async_computation | async-start | bytes 2097152 | tf_op jit(solution)/shard_map/all_to_all | solution.py:114
Sparse Core Ops, SparseCore 0:
  12.2 74.0 all-gather.4
  88.5 80.2 all-gather.8
  171.8 71.3 all-gather.6
  244.7 45.2 all-gather.10
where the time goes:
time: 303 us; the launch traced here: 302 us
  waiting for transfers between devices  187 us (62%)
  matrix products  56.7 us (19%)
  other arithmetic  21.1 us (7%)
  between operations  14.6 us (5%)
  local copies, waits for them, and re-layouts  13.9 us (5%)
  starting transfers between devices  6.04 us (2%)
    all_gather x1, waiting for transfers between devices, shards(): lax.all_gather(incoming, 'tensor', axis=3, tiled=True)[0, 0]  79.1 us
    ppermute x1, waiting for transfers between devices, passed_along(): lax.ppermute(array, axis, [(i, (i + by) % count) for i in range(count)])  47 us
    all_gather x1, waiting for transfers between devices, shards(): context_whole = lax.all_gather(context, 'tensor', axis=1, tiled=True)  38.3 us
    all_gather x2, waiting for transfers between devices, sent_together(): lax.all_gather(both, axis, axis=dim, tiled=True)  21.9 us
    dot_general x4, matrix products, one_block(): jnp.einsum('hqk,khd->qhd', probs, value_heads, preferred_element_type=jnp...  20.9 us
    sub x4, matrix products, one_block(): weights = jnp.exp(scores - highest)  20.8 us
    select_n x2, other arithmetic, placed(): return jnp.where(replacing, gathered[None], jnp.zeros_like(gathered[None]))  11.3 us
    dot_general x1, matrix products, shards(): jnp.dot(lax.all_gather(incoming, 'tensor', axis=3, tiled=True)[0, 0], w_j...  9.14 us
  transfers between devices with their start and end apart: 6, of which 5 were waited for; matrix products, arithmetic and copies ran while one was open for 26% of the time, Pallas kernels for 0%

commit v1 on v0

--- a/solution.py
+++ b/solution.py
@@ -110,7 +110,9 @@
     key_vals = projected[:, inner_local : 2 * inner_local].astype(jnp.bfloat16)
     value_vals = projected[:, 2 * inner_local :].astype(jnp.bfloat16)
     context = attend(queries, key_vals, value_vals, token_ids[0])
-    context_whole = lax.all_gather(context, "tensor", axis=1, tiled=True)
+    context_whole = jnp.concatenate(
+        lax.all_to_all(jnp.stack([context] * lax.axis_size("tensor")), "tensor", 0, 0), axis=1
+    )
     out_slice = lax.all_to_all(out_bf, "tensor", split_axis=0, concat_axis=1, tiled=True)
     update = lax.dot_general(
         context_whole, out_slice, (((1,), (1,)), ((), ())), preferred_element_type=jnp.float32

time: 303 us -> 319 us (1.053)
  matrix products: 56.7 us -> 67.8 us
  starting transfers between devices: 6.04 us -> 13 us
    all_gather x1 -> x0, waiting for transfers between devices: 38.3 us -> none  [shards(): context_whole = lax.all_gather(context, 'tensor', axis=1, tiled=True)]
    all_to_all x0 -> x1, waiting for transfers between devices: none -> 35.3 us  [shards(): lax.all_to_all(jnp.stack([context] * lax.axis_size('tensor')), 'tensor',...]
    sub x4, matrix products: 20.8 us -> 31.3 us  [one_block(): weights = jnp.exp(scores - highest)]
    all_to_all x0 -> x1, starting transfers between devices: none -> 5.04 us  [shards(): lax.all_to_all(jnp.stack([context] * lax.axis_size('tensor')), 'tensor',...]
  transfers between devices with their start and end apart: 6 -> 6, of which waited for: 5 -> 4; matrix products, arithmetic and copies ran while one was open for 26% -> 28% of each run, Pallas kernels for 0% -> 0%
where the time goes in v1:
time: 319 us
  waiting for transfers between devices  186 us (58%)
  matrix products  67.8 us (21%)
  other arithmetic  21.1 us (7%)
  between operations  14.6 us (5%)
  local copies, waits for them, and re-layouts  13.8 us (4%)
  starting transfers between devices  13 us (4%)
    all_gather x1, waiting for transfers between devices, shards(): lax.all_gather(incoming, 'tensor', axis=3, tiled=True)[0, 0]  81.5 us
    ppermute x1, waiting for transfers between devices, passed_along(): lax.ppermute(array, axis, [(i, (i + by) % count) for i in range(count)])  47 us
    all_to_all x1, waiting for transfers between devices, shards(): lax.all_to_all(jnp.stack([context] * lax.axis_size('tensor')), 'tensor',...  35.3 us
    sub x4, matrix products, one_block(): weights = jnp.exp(scores - highest)  31.3 us
    all_gather x2, waiting for transfers between devices, sent_together(): lax.all_gather(both, axis, axis=dim, tiled=True)  21.9 us
    dot_general x4, matrix products, one_block(): jnp.einsum('hqk,khd->qhd', probs, value_heads, preferred_element_type=jnp...  20.9 us
    select_n x2, other arithmetic, placed(): return jnp.where(replacing, gathered[None], jnp.zeros_like(gathered[None]))  11.3 us
    dot_general x1, matrix products, shards(): jnp.dot(lax.all_gather(incoming, 'tensor', axis=3, tiled=True)[0, 0], w_j...  9.45 us
  transfers between devices with their start and end apart: 6, of which 4 were waited for; matrix products, arithmetic and copies ran while one was open for 28% of the time, Pallas kernels for 0%

profile of v1, /device:TPU:1, one launch (start us, length us, event | category | flops | bytes accessed | tf_op | source)
XLA Modules:
  0.0 318.9 jit_solution(13650835602294083294)
XLA Ops:
  12.2 2.2 collective-permute-start
  14.3 47.0 %collective-permute-done = bf16[1,1,2048,512]{3,2,1,0:T(8,128)(2,1)S(1)} collective-permute-done((bf16[1,1,2048,512]{3,2,1,0:T(8,128)(2,1)}, bf16[1,1,2048,512]{3,2,1,0:T(8,128)(2,1)S(1)}, u32[]{:S(2)}, u32[]{:S(2)}) %collective-permute-start) | collective-permute-done | bytes 2097184 | tf_op jit(solution)/shard_map/ppermute | solution.py:23
  61.3 1.3 copy-done
  64.4 21.9 %all-gather.4.cloned.1.call-done = bf16[4,2048,256]{2,1,0:T(8,128)(2,1)} async-done(((bf16[4,256,256]{2,1,0:T(8,128)(2,1)}), bf16[4,2048,256]{2,1,0:T(8,128)(2,1)}) %all-gather.4.cloned.1.call-update) | async-done | bytes 4194320 | tf_op jit(solution)/shard_map/all_gather | solution.py:18
  86.3 3.8 %fusion.39 = (bf16[1,2048,256]{2,1,0:T(8,128)(2,1)}, bf16[2048,256]{1,0:T(8,128)(2,1)S(1)}, bf16[2048,256]{1,0:T(8,128)(2,1)S(1)}, bf16[2048,256]{1,0:T(8,128)(2,1)}) fusion(bf16[4,2048,256]{2,1,0:T(8,128)(2,1)} %all-gather.4.cloned.1.call-done), kind=kLoop, calls=%fused_computation.49 | loop fusion | bytes 8388608 | tf_op jit(solution)/shard_map/split | solution.py:18
  90.1 5.6 %all-to-all-start.1 = ((bf16[4,512,256]{2,1,0:T(8,128)(2,1)}), bf16[4,512,256]{2,1,0:T(8,128)(2,1)}, u32[]{:S(2)}, u32[]{:S(2)}) async-start(bf16[4,512,256]{2,1,0:T(8,128)(2,1)} %bitcast.21), calls=%async_computation.1 | async-start | bytes 2097152 | tf_op jit(solution)/shard_map/all_to_all | solution.py:116
  95.7 81.5 %all-gather.8.cloned.1.call-done = bf16[1,1,2048,2048]{3,2,1,0:T(8,128)(2,1)} async-done(((bf16[1,1,2048,512]{3,2,1,0:T(8,128)(2,1)}), bf16[1,1,2048,2048]{3,2,1,0:T(8,128)(2,1)}) %all-gather.8.cloned.1.call-update) | async-done | bytes 8388624 | tf_op jit(solution)/shard_map/all_gather | solution.py:105
  177.2 9.4 %fusion.23 = bf16[2048,768]{0,1:T(8,128)(2,1)S(1)} fusion(bf16[1,1,2048,2048]{3,2,1,0:T(8,128)(2,1)} %all-gather.8.cloned.1.call-done, bf16[2048,256]{1,0:T(8,128)(2,1)} %get-tuple-element.112, bf16[2048,256]{1,0:T(8,128)(2,1)S(1)} %get-tuple-element.111, bf16[2048,256]{1,0:T(8,128)(2,1)S(1)} %get-tuple-element.110), kind=kOutput, calls=%fused_computation.27 | convolution fusion | flops 6453460992 | bytes 14680064 | tf_op jit(solution)/shard_map/dot_general | solution.py:104
  187.9 1.3 copy.23
  189.2 62.4 %while.11 = (s32[]{:T(128)}, bf16[4,512,256]{2,1,0:T(8,128)(2,1)S(1)}, s32[2048]{0:T(1024)S(1)}, s32[4]{0:T(128)S(1)}, s32[2048]{0:T(1024)S(1)}, /*index=5*/bf16...) while((s32[]{:T(128)}, ...), condition=%wide.region_5.6_spmd.clone, body=%wide.region_2.5_spmd.clone.sunk | while | flops 1089603584 | bytes 23105728 | solution.py:62
  191.5 7.8 %fusion.54 = (f32[2,512]{1,0:T(2,128)S(1)}, f32[2,512,2048]{2,1,0:T(8,128)}) fusion(pred[512,2048]{1,0:T(8,128)(4,1)S(1)} %compare_and_fusion.2, bf16[512,2,128]{0,2,1:T(8,128)(2,1)S(1)} %bitcast.85, bf16[2048,2,128]{2,0,1:T(8,128)(2,1)} %get-tuple-element.207), kind=kOutput, calls=%fused_computation.48.clone.1 | convolution fusion | flops 545261568 | bytes 10752000 | tf_op jit(solution)/shard_map/while/body/eval_jaxpr/sub | solution.py:55
  199.4 5.2 %fusion.55 = bf16[2,512,128]{1,2,0:T(8,128)(2,1)S(1)} fusion(bf16[2048,2,128]{0,2,1:T(8,128)(2,1)} %get-tuple-element.208, f32[2,512,2048]{2,1,0:T(8,128)} %get-tuple-element.175, f32[2,512]{1,0:T(2,128)S(1)} %get-tuple-element.176), kind=kOutput, calls=%fused_computation.10.clone.1 | convolution fusion | flops 541196288 | bytes 9703424 | tf_op jit(solution)/shard_map/while/body/eval_jaxpr/hqk,khd->qhd/dot_general | solution.py:57
  207.2 7.8 %fusion.54 = (f32[2,512]{1,0:T(2,128)S(1)}, f32[2,512,2048]{2,1,0:T(8,128)}) fusion(pred[512,2048]{1,0:T(8,128)(4,1)S(1)} %compare_and_fusion.2, bf16[512,2,128]{0,2,1:T(8,128)(2,1)S(1)} %bitcast.85, bf16[2048,2,128]{2,0,1:T(8,128)(2,1)} %get-tuple-element.207), kind=kOutput, calls=%fused_computation.48.clone.1 | convolution fusion | flops 545261568 | bytes 10752000 | tf_op jit(solution)/shard_map/while/body/eval_jaxpr/sub | solution.py:55
  215.0 5.2 %fusion.55 = bf16[2,512,128]{1,2,0:T(8,128)(2,1)S(1)} fusion(bf16[2048,2,128]{0,2,1:T(8,128)(2,1)} %get-tuple-element.208, f32[2,512,2048]{2,1,0:T(8,128)} %get-tuple-element.175, f32[2,512]{1,0:T(2,128)S(1)} %get-tuple-element.176), kind=kOutput, calls=%fused_computation.10.clone.1 | convolution fusion | flops 541196288 | bytes 9703424 | tf_op jit(solution)/shard_map/while/body/eval_jaxpr/hqk,khd->qhd/dot_general | solution.py:57
  222.7 7.8 %fusion.54 = (f32[2,512]{1,0:T(2,128)S(1)}, f32[2,512,2048]{2,1,0:T(8,128)}) fusion(pred[512,2048]{1,0:T(8,128)(4,1)S(1)} %compare_and_fusion.2, bf16[512,2,128]{0,2,1:T(8,128)(2,1)S(1)} %bitcast.85, bf16[2048,2,128]{2,0,1:T(8,128)(2,1)} %get-tuple-element.207), kind=kOutput, calls=%fused_computation.48.clone.1 | convolution fusion | flops 545261568 | bytes 10752000 | tf_op jit(solution)/shard_map/while/body/eval_jaxpr/sub | solution.py:55
  230.5 5.3 %fusion.55 = bf16[2,512,128]{1,2,0:T(8,128)(2,1)S(1)} fusion(bf16[2048,2,128]{0,2,1:T(8,128)(2,1)} %get-tuple-element.208, f32[2,512,2048]{2,1,0:T(8,128)} %get-tuple-element.175, f32[2,512]{1,0:T(2,128)S(1)} %get-tuple-element.176), kind=kOutput, calls=%fused_computation.10.clone.1 | convolution fusion | flops 541196288 | bytes 9703424 | tf_op jit(solution)/shard_map/while/body/eval_jaxpr/hqk,khd->qhd/dot_general | solution.py:57
  238.3 7.8 %fusion.54 = (f32[2,512]{1,0:T(2,128)S(1)}, f32[2,512,2048]{2,1,0:T(8,128)}) fusion(pred[512,2048]{1,0:T(8,128)(4,1)S(1)} %compare_and_fusion.2, bf16[512,2,128]{0,2,1:T(8,128)(2,1)S(1)} %bitcast.85, bf16[2048,2,128]{2,0,1:T(8,128)(2,1)} %get-tuple-element.207), kind=kOutput, calls=%fused_computation.48.clone.1 | convolution fusion | flops 545261568 | bytes 10752000 | tf_op jit(solution)/shard_map/while/body/eval_jaxpr/sub | solution.py:55
  246.2 5.2 %fusion.55 = bf16[2,512,128]{1,2,0:T(8,128)(2,1)S(1)} fusion(bf16[2048,2,128]{0,2,1:T(8,128)(2,1)} %get-tuple-element.208, f32[2,512,2048]{2,1,0:T(8,128)} %get-tuple-element.175, f32[2,512]{1,0:T(2,128)S(1)} %get-tuple-element.176), kind=kOutput, calls=%fused_computation.10.clone.1 | convolution fusion | flops 541196288 | bytes 9703424 | tf_op jit(solution)/shard_map/while/body/eval_jaxpr/hqk,khd->qhd/dot_general | solution.py:57
  251.6 2.2 stack.3
  253.8 5.0 %all-to-all-start = ((bf16[4,2048,256]{2,1,0:T(8,128)(2,1)}), bf16[4,2048,256]{2,1,0:T(8,128)(2,1)}, u32[]{:S(2)}, u32[]{:S(2)}) async-start(bf16[4,2048,256]{2,1,0:T(8,128)(2,1)} %stack.3), calls=%async_computation | async-start | bytes 8388608 | tf_op jit(solution)/shard_map/all_to_all | solution.py:114
  259.5 5.7 %select_bitcast_fusion.4 = (f32[1,1,2048,256]{3,2,1,0:T(8,128)}, f32[1,1,2048,256]{3,2,1,0:T(8,128)}, f32[1,1,2048,256]{3,2,1,0:T(8,128)}, f32[1,1,2048,256]{3,2,1,0:T(8,128)}) fusion(pred[]{:T(512)S(6)} %eq.31, bf16[4,2048,256]{2,1,0:T(8,128)(2,1)} %all-gather.4.cloned.1.call-done), kind=kLoop, calls=%fused_computation.34 | loop fusion | flops 4194304 | bytes 12582913 | tf_op jit(solution)/shard_map/jit(_where)/select_n | solution.py:138
  265.2 5.7 %select_bitcast_fusion = (f32[1,1,2048,256]{3,2,1,0:T(8,128)}, f32[1,1,2048,256]{3,2,1,0:T(8,128)}, f32[1,1,2048,256]{3,2,1,0:T(8,128)}, f32[1,1,2048,256]{3,2,1,0:T(8,128)}) fusion(bf16[4,2048,256]{2,1,0:T(8,128)(2,1)} %all-gather.6.cloned.1.call-done, pred[]{:T(512)S(6)} %eq.31), kind=kLoop, calls=%fused_computation.30 | loop fusion | flops 4194304 | bytes 12582913 | tf_op jit(solution)/shard_map/jit(_where)/select_n | solution.py:138
  270.9 35.3 %all-to-all-done = bf16[4,2048,256]{2,1,0:T(8,128)(2,1)} async-done(((bf16[4,2048,256]{2,1,0:T(8,128)(2,1)}), bf16[4,2048,256]{2,1,0:T(8,128)(2,1)}, u32[]{:S(2)}, u32[]{:S(2)}) %all-to-all-start) | async-done | bytes 4194336 | tf_op jit(solution)/shard_map/all_to_all | solution.py:114
  306.1 6.2 %fusion.33 = bf16[1,1,2048,512]{3,2,1,0:T(8,128)(2,1)} fusion(bf16[4,2048,256]{2,1,0:T(8,128)(2,1)} %all-to-all-done, pred[]{:T(512)S(6)} %eq.31, bf16[4,512,256]{2,1,0:T(8,128)(2,1)} %all-to-all-done.1), kind=kOutput, calls=%fused_computation.29 | convolution fusion | flops 2149580800 | bytes 7340033 | tf_op jit(solution)/shard_map/dot_general | solution.py:117
  (67 shorter events, 15.1 us)
Async XLA Ops:
  7.2 55.5 %copy-start.1 = (f32[1,256,256]{2,1,0:T(8,128)S(1)}, f32[1,256,256]{2,1,0:T(8,128)}, u32[]{:S(2)}) copy-start(f32[1,256,256]{2,1,0:T(8,128)} %param.20) | copy-start | bytes 786436
  7.2 55.6 %copy-start.2 = (f32[1,256,256]{2,1,0:T(8,128)S(1)}, f32[1,256,256]{2,1,0:T(8,128)}, u32[]{:S(2)}) copy-start(f32[1,256,256]{2,1,0:T(8,128)} %param.21) | copy-start | bytes 786436
  7.2 55.6 %copy-start.3 = (f32[1,256,256]{2,1,0:T(8,128)S(1)}, f32[1,256,256]{2,1,0:T(8,128)}, u32[]{:S(2)}) copy-start(f32[1,256,256]{2,1,0:T(8,128)} %param.22) | copy-start | bytes 786436
  7.2 55.6 %copy-start.4 = (f32[1,256,256]{2,1,0:T(8,128)S(1)}, f32[1,256,256]{2,1,0:T(8,128)}, u32[]{:S(2)}) copy-start(f32[1,256,256]{2,1,0:T(8,128)} %param.23) | copy-start | bytes 786436
  7.2 56.5 %copy-start.5 = (s32[1,2048]{1,0:T(1,128)S(1)}, s32[1,2048]{1,0:T(1,128)}, u32[]{:S(2)}) copy-start(s32[1,2048]{1,0:T(1,128)} %param.14) | copy-start | bytes 24580
  7.2 79.1 %all-gather.4.cloned.1.call-start = ((), (), s32[]{:S(2)}) async-start(), calls=%async_computation.2 | async-start | bytes 4718592 | tf_op jit(solution)/shard_map/all_gather | solution.py:18
  12.1 165.1 %all-gather.8.cloned.1.call-start = ((), (), s32[]{:S(2)}) async-start(), calls=%async_computation.4 | async-start | bytes 10485760 | tf_op jit(solution)/shard_map/all_gather | solution.py:105
  12.2 49.2 %collective-permute-start = (bf16[1,1,2048,512]{3,2,1,0:T(8,128)(2,1)}, bf16[1,1,2048,512]{3,2,1,0:T(8,128)(2,1)S(1)}, u32[]{:S(2)}, u32[]{:S(2)}) collective-permute-start(bf16[1,1,2048,512]{3,2,1,0:T(8,128)(2,1)} %param.15), channel_id=1, source_target_pairs={{0,4},{4,8},{8,12},{12,0},{1,5},{5,9},{9,13},{13,1},{2,6},{6,10},{... | collective-permute-start | bytes 6291464 | tf_op jit(solution)/shard_map/ppermute | solution.py:23
  61.3 1.3 copy-start
  62.7 202.5 %all-gather.6.cloned.1.call-start = ((), (), s32[]{:S(2)}) async-start(), calls=%async_computation.3 | async-start | bytes 4718592 | tf_op jit(solution)/shard_map/all_gather | solution.py:18
  90.1 161.5 %all-to-all-start.1 = ((bf16[4,512,256]{2,1,0:T(8,128)(2,1)}), bf16[4,512,256]{2,1,0:T(8,128)(2,1)}, u32[]{:S(2)}, u32[]{:S(2)}) async-start(bf16[4,512,256]{2,1,0:T(8,128)(2,1)} %bitcast.21), calls=%async_computation.1 | async-start | bytes 2097152 | tf_op jit(solution)/shard_map/all_to_all | solution.py:116
  253.8 52.3 %all-to-all-start = ((bf16[4,2048,256]{2,1,0:T(8,128)(2,1)}), bf16[4,2048,256]{2,1,0:T(8,128)(2,1)}, u32[]{:S(2)}, u32[]{:S(2)}) async-start(bf16[4,2048,256]{2,1,0:T(8,128)(2,1)} %stack.3), calls=%async_computation | async-start | bytes 8388608 | tf_op jit(solution)/shard_map/all_to_all | solution.py:114
Sparse Core Ops, SparseCore 0:
  12.2 74.0 all-gather.3
  88.5 88.5 all-gather.7
  180.1 67.4 all-gather.5
